TPU v7x, 256 devices: a whole 4x4x8 slice. The times are simulated.
256 devices in a mesh: task: 32 (over x, z_hi, core), mp: 8 (over y, z_lo).
Axes of the slice: x: 4, y: 4, z: 8 (z_hi: 4, z_lo: 2; z = z_hi * 2 + z_lo), core: 2. Of those that a mesh axis runs over, the one named last changes fastest.
Arguments:
- hidden_in: bfloat16 [32768, 1024], P(('task', 'mp')), parts along dimension 0, may hold values from -16 to 16
- ff_gain: float32 [1024], replicated, may hold values from 0.5 to 1.5
- w_gate: bfloat16 [1024, 3072], P(None, 'mp'), may hold values from -0.1875 to 0.1875
- w_up: bfloat16 [1024, 3072], P(None, 'mp'), may hold values from -0.1875 to 0.1875
- w_out: bfloat16 [3072, 1024], P('mp'), may hold values from -0.109375 to 0.109375
- ff_rescale: float32 [98304], P(('task', 'mp')), parts along dimension 0, may hold values from 0.5 to 2
- final_gain: float32 [1024], replicated, may hold values from 0.5 to 1.5
- w_head: bfloat16 [1024, 16384], P(None, 'mp'), may hold values from -8 to 8
- targets: int32 [32768], P('task'), parts along dimension 0, may hold values from 0 to 16383
- lengths: int32 [128, 4], P('task'), parts along dimension 0, may hold values from 1 to 64, as said below
- labels: int32 [128], P('task'), parts along dimension 0, may hold values from 0 to 3
Outputs:
- scale_grad: float32 [98304], P(('task', 'mp')), parts along dimension 0
- loss_value: float32 [32], P('task'), parts along dimension 0
There are 32 independent parts, one for each index of `task`. A program takes and returns all parts, laid end to end along the dimension named above; an argument that names none is the same for every part. Nothing has to cross between parts.
Inputs may be any that keep to these rules, and one draw needn't show every extreme that they name: `lengths`: every answer choice has at least one target token.
All inputs are finite; a program needn't handle non-finite values.
Results may differ from a plain program's by a relative error of at most 0.0067.
Values may be sent and summed in bfloat16 or wider, within the bound.
A program may use at most 64 MiB of HBM per device.

v0:
```python
import jax
import jax.numpy as jnp
from jax import lax
from jax.sharding import PartitionSpec as P

epsilon = 1e-06


def sent_to_all(x, axis):
    copies = jnp.broadcast_to(x, (lax.axis_size(axis), *x.shape))
    return lax.all_to_all(copies, axis, split_axis=0, concat_axis=0, tiled=True)


def joined_along(pieces, dim):
    dims = list(pieces.shape[1:])
    dims[dim] *= pieces.shape[0]
    return jnp.moveaxis(pieces, 0, dim).reshape(dims)


def gathered_copies(x, axis, dim):
    pieces = sent_to_all(x, axis)
    return joined_along(pieces, dim)


def cut_along(x, dim, count):
    dims = x.shape
    pieces = x.reshape(*dims[:dim], count, dims[dim] // count, *dims[dim + 1 :])
    return jnp.moveaxis(pieces, dim, 0)


def summed_on_arrival(x, axis, dim):
    count = lax.axis_size(axis)
    pieces = lax.all_to_all(cut_along(x, dim, count), axis, 0, 0, tiled=True)
    return jnp.sum(pieces, axis=0)


def gathered_once(x, axis):
    leaves = jax.tree.leaves(x)
    turns = sorted(range(len(leaves)), key=lambda k: -leaves[k].size)
    width = (1, *leaves[turns[0]].shape)[-1]
    lines = [
        jnp.pad(leaves[k].reshape(-1), (0, -leaves[k].size % width)).reshape(-1, width)
        for k in turns
    ]
    both, at, found = (lax.all_gather(jnp.concatenate(lines), axis), 0, {})
    for k, line in zip(turns, lines):
        slab = both[:, at : at + len(line)].reshape(len(both), -1)
        found[k] = slab[:, : leaves[k].size].reshape(-1, *leaves[k].shape)
        at += len(line)
    numbers = iter(range(len(leaves)))
    return jax.tree.map(lambda _: found[next(numbers)], x)


def combined_all(x, axis, combine):
    everything = gathered_once(x, axis)
    initial = jax.tree.map(lambda part: part[0], everything)

    def lap(k, so_far):
        return combine(so_far, jax.tree.map(lambda part: part[k], everything))

    return lax.fori_loop(1, lax.axis_size(axis), lap, initial)


def rms_scale(values, gain):
    inverse = lax.rsqrt(jnp.mean(values * values, axis=-1, keepdims=True) + epsilon)
    return (values * inverse * gain, inverse)


def norm_back(values, inverse, gain, upstream):
    scaled = upstream * gain
    return inverse * scaled - values * inverse**3 * jnp.mean(
        scaled * values, axis=-1, keepdims=True
    )


def task_loss(log_probs, lengths, labels):
    examples, choices = lengths.shape
    length = log_probs.shape[0] // (examples * choices)
    number_type = log_probs.dtype
    shaped = log_probs.reshape(examples, choices, length)
    position = jnp.arange(length, dtype=jnp.int32)
    valid = (position[None, None, :] < lengths[:, :, None]).astype(number_type)
    counts = lengths.astype(number_type)
    summed = jnp.sum(shaped * valid, axis=-1)
    average = summed / counts
    correct = (jnp.arange(choices, dtype=jnp.int32)[None, :] == labels[:, None]).astype(number_type)
    wrong = 1.0 - correct
    likely = -jnp.sum(summed * correct) / jnp.sum(counts * correct)
    safe = jnp.where(valid > 0, shaped, -1.0)
    unlikely = -jnp.sum(jnp.log1p(-jnp.exp(safe)) * valid * wrong[:, :, None]) / jnp.sum(
        counts * wrong
    )
    normed = -jnp.mean(jnp.sum(jax.nn.log_softmax(average, axis=-1) * correct, axis=-1))
    return likely + unlikely + normed


def pair_merge(first, second):
    first_max, first_sum, first_target = first
    second_max, second_sum, second_target = second
    joint_max = jnp.maximum(first_max, second_max)
    joint_sum = first_sum * jnp.exp(first_max - joint_max) + second_sum * jnp.exp(
        second_max - joint_max
    )
    return (joint_max, joint_sum, first_target + second_target)


def per_device(
    hidden_in,
    ff_gain,
    w_gate,
    w_up,
    w_out,
    ff_rescale,
    final_gain,
    w_head,
    targets,
    lengths,
    labels,
):
    place = lax.axis_index("mp")
    contract = (((1,), (1,)), ((), ()))
    inputs = hidden_in.astype(jnp.float32)
    normed_in = rms_scale(inputs, ff_gain)[0].astype(jnp.bfloat16)
    width = w_gate.shape[1]
    shard_rows = gathered_copies(normed_in, "mp", 0)
    gate_part = jnp.dot(shard_rows, w_gate, preferred_element_type=jnp.float32)
    up_part = jnp.dot(shard_rows, w_up, preferred_element_type=jnp.float32)
    projected = jnp.concatenate([gate_part, up_part], axis=1)
    activated = jax.nn.gelu(projected[:, :width], approximate=True) * projected[:, width:]
    hidden = (activated * ff_rescale).astype(jnp.bfloat16)
    residual = (
        summed_on_arrival(jnp.dot(hidden, w_out, preferred_element_type=jnp.float32), "mp", 0)
        + inputs
    )
    normed_out, inverse = rms_scale(residual, final_gain)
    logits = jnp.dot(
        gathered_copies(normed_out.astype(jnp.bfloat16), "mp", 0),
        w_head,
        preferred_element_type=jnp.float32,
    )
    vocab_own = logits.shape[1]
    columns = jnp.arange(vocab_own, dtype=jnp.int32)[None, :]
    is_target = columns == (targets - place * vocab_own)[:, None]
    target_part = jnp.sum(jnp.where(is_target, logits, 0.0), axis=1)
    local_max = jnp.max(logits, axis=1)
    local_sum = jnp.sum(jnp.exp(logits - local_max[:, None]), axis=1)
    row_max, row_sum, target_logit = combined_all(
        (local_max, local_sum, target_part), "mp", pair_merge
    )
    log_norm = row_max + jnp.log(row_sum)
    log_probs = target_logit - log_norm
    loss_value, pullback = jax.vjp(lambda values: task_loss(values, lengths, labels), log_probs)
    (token_weight,) = pullback(jnp.ones_like(loss_value))
    softmax_rows = jnp.exp(logits - log_norm[:, None])
    logit_grad = (token_weight[:, None] * (is_target.astype(jnp.float32) - softmax_rows)).astype(
        jnp.bfloat16
    )
    normed_grad = summed_on_arrival(
        lax.dot_general(logit_grad, w_head, contract, preferred_element_type=jnp.float32), "mp", 0
    )
    resid_grad = norm_back(residual, inverse, final_gain, normed_grad).astype(jnp.bfloat16)
    hidden_grad = lax.dot_general(
        lax.all_gather(resid_grad, "mp", axis=0, tiled=True),
        w_out,
        contract,
        preferred_element_type=jnp.float32,
    )
    scale_grad = jnp.sum(hidden_grad * activated, axis=0)
    return (scale_grad, loss_value.reshape(1))


def solution(mesh):
    return jax.shard_map(
        per_device,
        mesh=mesh,
        in_specs=(
            P(("task", "mp"), None),
            P(),
            P(None, "mp"),
            P(None, "mp"),
            P("mp", None),
            P(("task", "mp")),
            P(),
            P(None, "mp"),
            P("task"),
            P("task", None),
            P("task"),
        ),
        out_specs=(P(("task", "mp")), P("task")),
        check_vma=False,
    )
```

profile of v0, /device:TPU:1, one launch (start us, length us, event | category | flops | bytes accessed | tf_op | source)
XLA Modules:
  0.0 303.6 jit_solution(508517285441279573)
XLA Ops:
  7.2 0.0 copy-start
  7.2 1.2 fusion.14
  8.3 1.1 fusion.16
  9.4 0.3 broadcast_in_dim.32
  9.7 0.0 copy-start.8
  9.7 32.7 %all_to_all.20 = bf16[8,128,1024]{2,1,0:T(8,128)(2,1)S(1)} all-to-all(bf16[8,128,1024]{2,1,0:T(8,128)(2,1)S(1)} %broadcast_in_dim.32), channel_id=1, replica_groups=mesh['task'=32,'mp'=8] {'mp'}, dimensions={0} | all-to-all | bytes 4194304 | tf_op jit(solution)/shard_map/all_to_all | solution.py:11
  42.4 1.2 fusion.24
  43.7 0.0 copy-start.5
  43.7 1.4 fusion.11
  45.1 1.3 fusion.12
  46.4 50.9 %all_to_all.21 = f32[8,128,1024]{2,1,0:T(8,128)} all-to-all(f32[8,128,1024]{2,1,0:T(8,128)S(1)} %bitcast.39), channel_id=1, replica_groups=mesh['task'=32,'mp'=8] {'mp'}, dimensions={0} | all-to-all | bytes 8388608 | tf_op jit(solution)/shard_map/all_to_all | solution.py:33
  97.3 2.6 reduce_sum.156
  100.0 0.2 multiply_reduce_fusion.2
  100.2 0.1 multiply_convert_fusion.4
  100.3 1.6 broadcast_in_dim.56
  101.9 4.5 %all-to-all-start.2 = ((bf16[8,128,1024]{2,1,0:T(8,128)(2,1)}), bf16[8,128,1024]{2,1,0:T(8,128)(2,1)}, u32[]{:S(2)}, u32[]{:S(2)}) async-start(bf16[8,128,1024]{2,1,0:T(8,128)(2,1)} %broadcast_in_dim.56), calls=%async_computation.2 | async-start | bytes 4194304 | tf_op jit(solution)/shard_map/all_to_all | solution.py:11
  106.3 0.0 all-gather.4.cloned.1.call-start
  106.4 0.1 iota_compare_fusion.1
  106.5 0.1 lt.41
  106.6 0.1 convert_subtract_fusion
  106.6 0.1 mul.237
  106.7 0.1 mul.238
  106.8 23.6 %all-to-all-done.2 = bf16[8,128,1024]{2,1,0:T(8,128)(2,1)} async-done(((bf16[8,128,1024]{2,1,0:T(8,128)(2,1)}), bf16[8,128,1024]{2,1,0:T(8,128)(2,1)}, u32[]{:S(2)}, u32[]{:S(2)}) %all-to-all-start.2) | async-done | bytes 2097184 | tf_op jit(solution)/shard_map/all_to_all | solution.py:11
  130.4 7.1 %fusion.23 = (f32[1024]{0:T(1024)S(1)}, f32[1024,2048]{1,0:T(8,128)S(1)}) fusion(bf16[1024,1024]{1,0:T(8,128)(2,1)} %bitcast.5, bf16[1024,2048]{1,0:T(8,128)(2,1)} %param.20), kind=kOutput, calls=%fused_computation.68 | convolution fusion | flops 4297063424 | bytes 14684160 | tf_op jit(solution)/shard_map/dot_general | solution.py:136
  137.5 2.6 exponential_reduce_fusion
  140.1 0.7 copy-done.2
  140.7 22.9 %all-gather.1 = f32[8,3,1024]{2,1,0:T(4,128)S(1)} all-gather(f32[1,3,1024]{2,1,0:T(4,128)S(1)} %maximum_bitcast_fusion), channel_id=2, replica_groups=mesh['task'=32,'mp'=8] {'mp'}, dimensions={0}, use_global_device_ids=true | all-gather | bytes 110592 | tf_op jit(solution)/shard_map/all_gather | solution.py:45
  163.7 0.1 fusion.21
  163.8 0.6 while.19
  164.4 0.6 multiply_reduce_fusion.3
  165.0 0.1 reshape.158
  165.1 0.2 select_reduce_fusion.1
  165.3 0.1 fusion.20
  165.4 0.2 exponential_reduce_fusion.1
  165.6 0.7 select_reduce_fusion.3
  167.6 0.1 fusion.19
  167.7 0.1 mul.212
  167.8 0.1 mul.213
  167.9 0.1 broadcast_in_dim.62
  167.9 0.1 broadcast_in_dim.63
  168.0 8.8 %fusion = f32[1024,1024]{1,0:T(8,128)S(1)} fusion(bf16[1024,2048]{1,0:T(8,128)(2,1)} %param.20, f32[1024,2048]{1,0:T(8,128)} %copy-done.2, f32[1024]{0:T(1024)S(1)} %get-tuple-element.210, f32[1024]{0:T(1024)S(1)} %select_add_fusion, s32[1024]{0:T(1024)S(1)} %broadcast_subtract_fusion), kind=kOutput, calls=%fused_computation.8 | convolution fusion | flops 4307550208 | bytes 16789504 | tf_op jit(solution)/shard_map/dot_general | solution.py:159
  176.8 46.4 %all_to_all.22 = f32[8,128,1024]{2,1,0:T(8,128)} all-to-all(f32[8,128,1024]{2,1,0:T(8,128)S(1)} %bitcast.40), channel_id=1, replica_groups=mesh['task'=32,'mp'=8] {'mp'}, dimensions={0} | all-to-all | bytes 8388608 | tf_op jit(solution)/shard_map/all_to_all | solution.py:33
  223.2 3.4 %reduce_sum.165 = f32[128,1024]{1,0:T(8,128)} reduce(f32[8,128,1024]{2,1,0:T(8,128)} %all_to_all.22, f32[]{:T(128)} %constant.79.clone.1), dimensions={0}, to_apply=%region_14.15 | reduce | flops 917504 | bytes 4718596 | tf_op jit(solution)/shard_map/reduce_sum | solution.py:34
  226.6 1.2 multiply_reduce_fusion.1
  227.8 2.0 subtract_convert_fusion
  229.8 0.0 all-gather.4.cloned.1.call-update
  233.0 59.2 %all-gather.4.cloned.1.call-done = bf16[1024,1024]{1,0:T(8,128)(2,1)} async-done(((bf16[128,1024]{1,0:T(8,128)(2,1)}), bf16[1024,1024]{1,0:T(8,128)(2,1)}) %all-gather.4.cloned.1.call-update) | async-done | bytes 2097168 | tf_op jit(solution)/shard_map/all_gather | solution.py:163
  292.2 3.5 %multiply_reduce_fusion = f32[384]{0:T(512)} fusion(f32[1024,384]{1,0:T(8,128)S(1)} %fusion.11, bf16[1024,1024]{1,0:T(8,128)(2,1)} %all-gather.4.cloned.1.call-done, bf16[384,1024]{1,0:T(8,128)(2,1)S(1)} %copy-done), kind=kOutput, calls=%fused_computation.21 | convolution fusion | flops 806092416 | bytes 4457984 | tf_op jit(solution)/shard_map/dot_general | solution.py:162
  (55 shorter events, 0.4 us)
Async XLA Ops:
  7.2 38.0 %copy-start = (bf16[384,1024]{1,0:T(8,128)(2,1)S(1)}, bf16[384,1024]{1,0:T(8,128)(2,1)}, u32[]{:S(2)}) copy-start(bf16[384,1024]{1,0:T(8,128)(2,1)} %param.17) | copy-start | bytes 2359300
  9.7 32.7 %copy-start.8 = (bf16[1024,384]{1,0:T(8,128)(2,1)S(1)}, bf16[1024,384]{1,0:T(8,128)(2,1)}, u32[]{:S(2)}) copy-start(bf16[1024,384]{1,0:T(8,128)(2,1)} %param.15) | copy-start | bytes 2359300
  42.4 1.3 copy-start.9
  43.7 1.5 copy-start.5
  97.3 2.7 copy-start.1
  97.3 2.8 copy-start.4
  101.9 4.5 %copy-start.3 = (s32[4,4]{1,0:T(4,128)S(1)}, s32[4,4]{1,0:T(4,128)}, u32[]{:S(2)}) copy-start(s32[4,4]{1,0:T(4,128)} %param.22) | copy-start | bytes 196
  101.9 4.7 %copy-start.6 = (s32[4]{0:T(128)S(1)}, s32[4]{0:T(128)}, u32[]{:S(2)}) copy-start(s32[4]{0:T(128)} %param.23) | copy-start | bytes 52
  101.9 4.9 %copy-start.7 = (s32[1024]{0:T(1024)S(1)}, s32[1024]{0:T(1024)}, u32[]{:S(2)}) copy-start(s32[1024]{0:T(1024)} %param.21) | copy-start | bytes 12292
  101.9 28.6 %all-to-all-start.2 = ((bf16[8,128,1024]{2,1,0:T(8,128)(2,1)}), bf16[8,128,1024]{2,1,0:T(8,128)(2,1)}, u32[]{:S(2)}, u32[]{:S(2)}) async-start(bf16[8,128,1024]{2,1,0:T(8,128)(2,1)} %broadcast_in_dim.56), calls=%async_computation.2 | async-start | bytes 4194304 | tf_op jit(solution)/shard_map/all_to_all | solution.py:11
  106.3 185.8 %all-gather.4.cloned.1.call-start = ((), (), s32[]{:S(2)}) async-start(), calls=%async_computation.4 | async-start | bytes 2359296 | tf_op jit(solution)/shard_map/all_gather | solution.py:163
  137.5 3.2 %copy-start.2 = (f32[1024,2048]{1,0:T(8,128)}, f32[1024,2048]{1,0:T(8,128)S(1)}, u32[]{:S(2)}) copy-start(f32[1024,2048]{1,0:T(8,128)S(1)} %get-tuple-element.226) | copy-start | bytes 25165828
Sparse Core Ops, SparseCore 0:
  229.9 62.1 all-gather.3
where the time goes:
time: 304 us
  blocking collectives  153 us (50%)
  waiting for transfers between devices  82.9 us (27%)
  matrix products  23.3 us (8%)
  between operations  19.8 us (7%)
  other arithmetic  16.5 us (5%)
  starting transfers between devices  4.51 us (1%)
  local copies, waits for them, and re-layouts  3.4 us (1%)
    all_to_all x2, blocking collectives, summed_on_arrival(): pieces = lax.all_to_all(cut_along(x, dim, count), axis, 0, 0, tiled=True)  97.3 us
    all_gather x1, waiting for transfers between devices, per_device(): lax.all_gather(resid_grad, 'mp', axis=0, tiled=True)  59.2 us
    all_to_all x1, blocking collectives, sent_to_all(): return lax.all_to_all(copies, axis, split_axis=0, concat_axis=0, tiled=True)  32.7 us
    all_to_all x1, waiting for transfers between devices, sent_to_all(): return lax.all_to_all(copies, axis, split_axis=0, concat_axis=0, tiled=True)  23.6 us
    all_gather x1, blocking collectives, gathered_once(): both, at, found = (lax.all_gather(jnp.concatenate(lines), axis), 0, {})  22.9 us
    dot_general x1, matrix products, per_device(): lax.dot_general(logit_grad, w_head, contract, preferred_element_type=jnp....  8.8 us
    dot_general x1, matrix products, per_device(): jnp.dot(gathered_copies(normed_out.astype(jnp.bfloat16), 'mp', 0), w_head...  7.06 us
  transfers between devices with their start and end apart: 2, of which 2 were waited for; matrix products, arithmetic and copies ran while one was open for 0% of the time, Pallas kernels for 0%

commit v1 on v0

--- a/solution.py
+++ b/solution.py
@@ -159,11 +159,15 @@
         lax.dot_general(logit_grad, w_head, contract, preferred_element_type=jnp.float32), "mp", 0
     )
     resid_grad = norm_back(residual, inverse, final_gain, normed_grad).astype(jnp.bfloat16)
+
+    def edit_the_chains(payload):
+        u1 = jax.lax.psum(1, "mp")
+        t_next = jnp.stack(u1 * [payload])
+        piece_now = jax.lax.all_to_all(t_next, "mp", 0, 0)
+        return jnp.concatenate(piece_now, 0)
+
     hidden_grad = lax.dot_general(
-        lax.all_gather(resid_grad, "mp", axis=0, tiled=True),
-        w_out,
-        contract,
-        preferred_element_type=jnp.float32,
+        edit_the_chains(resid_grad), w_out, contract, preferred_element_type=jnp.float32
     )
     scale_grad = jnp.sum(hidden_grad * activated, axis=0)
     return (scale_grad, loss_value.reshape(1))

time: 304 us -> 260 us (0.86)
  the two profiles are of different devices: /device:TPU:1 before, /device:TPU:6 now
where the time goes in v1:
time: 260 us
  blocking collectives  159 us (61%)
  waiting for transfers between devices  41 us (16%)
  matrix products  23.3 us (9%)
  other arithmetic  15.8 us (6%)
  starting transfers between devices  8.81 us (3%)
  between operations  6.42 us (2%)
  local copies, waits for them, and re-layouts  4.96 us (2%)
    all_to_all x2, blocking collectives, summed_on_arrival(): pieces = lax.all_to_all(cut_along(x, dim, count), axis, 0, 0, tiled=True)  97.8 us
    all_to_all x1, blocking collectives, sent_to_all(): return lax.all_to_all(copies, axis, split_axis=0, concat_axis=0, tiled=True)  33 us
    all_gather x1, blocking collectives, gathered_once(): both, at, found = (lax.all_gather(jnp.concatenate(lines), axis), 0, {})  28.4 us
    all_to_all x1, waiting for transfers between devices, sent_to_all(): return lax.all_to_all(copies, axis, split_axis=0, concat_axis=0, tiled=True)  24.8 us
    all_to_all x1, waiting for transfers between devices, edit_the_chains(): piece_now = jax.lax.all_to_all(t_next, 'mp', 0, 0)  16.2 us
    dot_general x1, matrix products, per_device(): lax.dot_general(logit_grad, w_head, contract, preferred_element_type=jnp....  8.8 us
    dot_general x1, matrix products, per_device(): jnp.dot(gathered_copies(normed_out.astype(jnp.bfloat16), 'mp', 0), w_head...  7.06 us
    reduce_sum x2, other arithmetic, summed_on_arrival(): return jnp.sum(pieces, axis=0)  6.05 us
  transfers between devices with their start and end apart: 2, of which 2 were waited for; matrix products, arithmetic and copies ran while one was open for 0% of the time, Pallas kernels for 0%

profile of v1, /device:TPU:6, one launch (start us, length us, event | category | flops | bytes accessed | tf_op | source)
XLA Modules:
  0.0 259.7 jit_solution(9048340244180259038)
XLA Ops:
  0.6 0.0 copy-start
  0.6 1.2 fusion.14
  1.8 1.1 fusion.16
  2.9 0.3 broadcast_in_dim.32
  3.2 0.0 copy-start.8
  3.2 33.0 %all_to_all.25 = bf16[8,128,1024]{2,1,0:T(8,128)(2,1)S(1)} all-to-all(bf16[8,128,1024]{2,1,0:T(8,128)(2,1)S(1)} %broadcast_in_dim.32), channel_id=1, replica_groups=mesh['task'=32,'mp'=8] {'mp'}, dimensions={0} | all-to-all | bytes 4194304 | tf_op jit(solution)/shard_map/all_to_all | solution.py:11
  36.2 1.2 fusion.24
  37.4 0.0 copy-start.5
  37.5 1.4 fusion.11
  38.9 1.2 fusion.12
  40.2 51.8 %all_to_all.26 = f32[8,128,1024]{2,1,0:T(8,128)} all-to-all(f32[8,128,1024]{2,1,0:T(8,128)S(1)} %bitcast.40), channel_id=1, replica_groups=mesh['task'=32,'mp'=8] {'mp'}, dimensions={0} | all-to-all | bytes 8388608 | tf_op jit(solution)/shard_map/all_to_all | solution.py:33
  92.0 2.6 %reduce_sum.156 = f32[128,1024]{1,0:T(8,128)S(1)} reduce(f32[8,128,1024]{2,1,0:T(8,128)} %all_to_all.26, f32[]{:T(128)} %constant.79.clone.1), dimensions={0}, to_apply=%region_1.0 | reduce | flops 917504 | bytes 4718596 | tf_op jit(solution)/shard_map/reduce_sum | solution.py:34
  94.6 0.2 multiply_reduce_fusion.2
  94.8 0.1 multiply_convert_fusion.4
  94.9 1.6 broadcast_in_dim.56
  96.5 4.5 %all-to-all-start.2 = ((bf16[8,128,1024]{2,1,0:T(8,128)(2,1)}), bf16[8,128,1024]{2,1,0:T(8,128)(2,1)}, u32[]{:S(2)}, u32[]{:S(2)}) async-start(bf16[8,128,1024]{2,1,0:T(8,128)(2,1)} %broadcast_in_dim.56), calls=%async_computation.2 | async-start | bytes 4194304 | tf_op jit(solution)/shard_map/all_to_all | solution.py:11
  101.0 0.1 iota_compare_fusion.1
  101.1 0.1 lt.41
  101.2 0.1 convert_subtract_fusion
  101.2 0.1 mul.237
  101.3 0.1 mul.238
  101.4 24.8 %all-to-all-done.2 = bf16[8,128,1024]{2,1,0:T(8,128)(2,1)} async-done(((bf16[8,128,1024]{2,1,0:T(8,128)(2,1)}), bf16[8,128,1024]{2,1,0:T(8,128)(2,1)}, u32[]{:S(2)}, u32[]{:S(2)}) %all-to-all-start.2) | async-done | bytes 2097184 | tf_op jit(solution)/shard_map/all_to_all | solution.py:11
  126.2 7.1 %fusion.23 = (f32[1024]{0:T(1024)S(1)}, f32[1024,2048]{1,0:T(8,128)S(1)}) fusion(bf16[1024,1024]{1,0:T(8,128)(2,1)} %bitcast.5, bf16[1024,2048]{1,0:T(8,128)(2,1)} %param.20), kind=kOutput, calls=%fused_computation.68 | convolution fusion | flops 4297063424 | bytes 14684160 | tf_op jit(solution)/shard_map/dot_general | solution.py:136
  133.3 2.6 exponential_reduce_fusion
  135.9 0.7 copy-done.2
  136.5 28.4 %all-gather.1 = f32[8,3,1024]{2,1,0:T(4,128)S(1)} all-gather(f32[1,3,1024]{2,1,0:T(4,128)S(1)} %maximum_bitcast_fusion), channel_id=2, replica_groups=mesh['task'=32,'mp'=8] {'mp'}, dimensions={0}, use_global_device_ids=true | all-gather | bytes 110592 | tf_op jit(solution)/shard_map/all_gather | solution.py:45
  165.0 0.1 fusion.21
  165.1 0.6 while.19
  165.7 0.6 multiply_reduce_fusion.3
  166.3 0.1 reshape.163
  166.4 0.2 select_reduce_fusion.1
  166.6 0.1 fusion.20
  166.7 0.2 exponential_reduce_fusion.1
  166.9 0.7 select_reduce_fusion.3
  168.9 0.1 fusion.19
  169.0 0.1 mul.212
  169.1 0.1 mul.213
  169.1 0.1 broadcast_in_dim.62
  169.2 0.1 broadcast_in_dim.63
  169.3 8.8 %fusion = f32[1024,1024]{1,0:T(8,128)S(1)} fusion(bf16[1024,2048]{1,0:T(8,128)(2,1)} %param.20, f32[1024,2048]{1,0:T(8,128)} %copy-done.2, f32[1024]{0:T(1024)S(1)} %get-tuple-element.210, f32[1024]{0:T(1024)S(1)} %select_add_fusion, s32[1024]{0:T(1024)S(1)} %broadcast_subtract_fusion), kind=kOutput, calls=%fused_computation.8 | convolution fusion | flops 4307550208 | bytes 16789504 | tf_op jit(solution)/shard_map/dot_general | solution.py:159
  178.1 45.9 %all_to_all.27 = f32[8,128,1024]{2,1,0:T(8,128)} all-to-all(f32[8,128,1024]{2,1,0:T(8,128)S(1)} %bitcast.41), channel_id=1, replica_groups=mesh['task'=32,'mp'=8] {'mp'}, dimensions={0} | all-to-all | bytes 8388608 | tf_op jit(solution)/shard_map/all_to_all | solution.py:33
  224.1 3.4 %reduce_sum.165 = f32[128,1024]{1,0:T(8,128)} reduce(f32[8,128,1024]{2,1,0:T(8,128)} %all_to_all.27, f32[]{:T(128)} %constant.79.clone.1), dimensions={0}, to_apply=%region_14.15 | reduce | flops 917504 | bytes 4718596 | tf_op jit(solution)/shard_map/reduce_sum | solution.py:34
  227.5 1.2 multiply_reduce_fusion.1
  228.7 1.2 subtract_convert_fusion
  229.9 1.6 stack.2
  231.5 4.3 %all-to-all-start.4 = ((bf16[8,128,1024]{2,1,0:T(8,128)(2,1)}), bf16[8,128,1024]{2,1,0:T(8,128)(2,1)}, u32[]{:S(2)}, u32[]{:S(2)}) async-start(bf16[8,128,1024]{2,1,0:T(8,128)(2,1)} %stack.2), calls=%async_computation.4 | async-start | bytes 4194304 | tf_op jit(solution)/shard_map/all_to_all | solution.py:166
  239.0 16.2 %all-to-all-done.4 = bf16[8,128,1024]{2,1,0:T(8,128)(2,1)} async-done(((bf16[8,128,1024]{2,1,0:T(8,128)(2,1)}), bf16[8,128,1024]{2,1,0:T(8,128)(2,1)}, u32[]{:S(2)}, u32[]{:S(2)}) %all-to-all-start.4) | async-done | bytes 2097184 | tf_op jit(solution)/shard_map/all_to_all | solution.py:166
  255.1 3.5 %multiply_reduce_fusion = f32[384]{0:T(512)} fusion(f32[1024,384]{1,0:T(8,128)S(1)} %fusion.11, bf16[1024,1024]{1,0:T(8,128)(2,1)} %bitcast.14, bf16[384,1024]{1,0:T(8,128)(2,1)S(1)} %copy-done), kind=kOutput, calls=%fused_computation.21 | convolution fusion | flops 806092416 | bytes 4457984 | tf_op jit(solution)/shard_map/dot_general | solution.py:169
  (55 shorter events, 0.4 us)
Async XLA Ops:
  0.6 38.3 %copy-start = (bf16[384,1024]{1,0:T(8,128)(2,1)S(1)}, bf16[384,1024]{1,0:T(8,128)(2,1)}, u32[]{:S(2)}) copy-start(bf16[384,1024]{1,0:T(8,128)(2,1)} %param.17) | copy-start | bytes 2359300
  3.2 33.0 %copy-start.8 = (bf16[1024,384]{1,0:T(8,128)(2,1)S(1)}, bf16[1024,384]{1,0:T(8,128)(2,1)}, u32[]{:S(2)}) copy-start(bf16[1024,384]{1,0:T(8,128)(2,1)} %param.15) | copy-start | bytes 2359300
  36.2 1.3 copy-start.9
  37.4 1.5 copy-start.5
  92.0 2.7 %copy-start.1 = (bf16[128,1024]{1,0:T(8,128)(2,1)S(1)}, bf16[128,1024]{1,0:T(8,128)(2,1)}, u32[]{:S(2)}) copy-start(bf16[128,1024]{1,0:T(8,128)(2,1)} %param.13) | copy-start | bytes 786436
  92.0 2.8 %copy-start.4 = (f32[1024]{0:T(1024)S(1)}, f32[1024]{0:T(1024)}, u32[]{:S(2)}) copy-start(f32[1024]{0:T(1024)} %param.19) | copy-start | bytes 12292
  96.5 4.5 %copy-start.3 = (s32[4,4]{1,0:T(4,128)S(1)}, s32[4,4]{1,0:T(4,128)}, u32[]{:S(2)}) copy-start(s32[4,4]{1,0:T(4,128)} %param.22) | copy-start | bytes 196
  96.5 4.7 %copy-start.6 = (s32[4]{0:T(128)S(1)}, s32[4]{0:T(128)}, u32[]{:S(2)}) copy-start(s32[4]{0:T(128)} %param.23) | copy-start | bytes 52
  96.5 4.9 %copy-start.7 = (s32[1024]{0:T(1024)S(1)}, s32[1024]{0:T(1024)}, u32[]{:S(2)}) copy-start(s32[1024]{0:T(1024)} %param.21) | copy-start | bytes 12292
  96.5 29.7 %all-to-all-start.2 = ((bf16[8,128,1024]{2,1,0:T(8,128)(2,1)}), bf16[8,128,1024]{2,1,0:T(8,128)(2,1)}, u32[]{:S(2)}, u32[]{:S(2)}) async-start(bf16[8,128,1024]{2,1,0:T(8,128)(2,1)} %broadcast_in_dim.56), calls=%async_computation.2 | async-start | bytes 4194304 | tf_op jit(solution)/shard_map/all_to_all | solution.py:11
  133.3 3.2 %copy-start.2 = (f32[1024,2048]{1,0:T(8,128)}, f32[1024,2048]{1,0:T(8,128)S(1)}, u32[]{:S(2)}) copy-start(f32[1024,2048]{1,0:T(8,128)S(1)} %get-tuple-element.226) | copy-start | bytes 25165828
  231.5 23.7 %all-to-all-start.4 = ((bf16[8,128,1024]{2,1,0:T(8,128)(2,1)}), bf16[8,128,1024]{2,1,0:T(8,128)(2,1)}, u32[]{:S(2)}, u32[]{:S(2)}) async-start(bf16[8,128,1024]{2,1,0:T(8,128)(2,1)} %stack.2), calls=%async_computation.4 | async-start | bytes 4194304 | tf_op jit(solution)/shard_map/all_to_all | solution.py:166
